TPU v7x, 256 devices: a whole 4x4x8 slice. The times are simulated.
256 devices in a mesh: crop: 4 (over z_hi, core), row: 64 (over y, x, z_lo).
Axes of the slice: x: 4, y: 4, z: 8 (z_hi: 2, z_lo: 4; z = z_hi * 4 + z_lo), core: 2. Of those that a mesh axis runs over, the one named last changes fastest.
Arguments:
- pair: bfloat16 [4, 512, 512, 128], P('crop', 'row'), may hold values from -6 to 6
- cotangent: bfloat16 [4, 512, 512, 128], P('crop', 'row'), may hold values from -6 to 6
- lengths: int32 [4], P('crop'), may hold values from 256 to 512
- proj_weight: bfloat16 [128, 640], replicated, may hold values from -0.5 to 0.5
- out_weight: bfloat16 [128, 128], replicated, may hold values from -0.5 to 0.5
- up_weight: bfloat16 [128, 512], replicated, may hold values from -0.5 to 0.5
- down_weight: bfloat16 [512, 128], replicated, may hold values from -0.25 to 0.25
- norm_gain: float32 [3, 128], replicated, may hold values from 0.1 to 1.9
- norm_bias: float32 [3, 128], replicated, may hold values from -3 to 3
Outputs:
- grad_pair: bfloat16 [4, 512, 512, 128], P('crop', 'row')
- grad_proj: float32 [128, 640], replicated
- grad_out: float32 [128, 128], replicated
- grad_up: float32 [128, 512], replicated
- grad_down: float32 [512, 128], replicated
- grad_gain: float32 [3, 128], replicated
- grad_bias: float32 [3, 128], replicated
Inputs may be any that keep to these rules, and one draw needn't show every extreme that they name: lengths[s] residues of crop s are present; the rest are masked.
All inputs are finite; a program needn't handle non-finite values.
Results may differ from a plain program's by a relative error of at most 0.009.
Values may be sent and summed in bfloat16 or wider, within the bound.
A program may use at most 128 MiB of HBM per device.

v0:
```python
import jax
import jax.numpy as jnp
from jax import lax
from jax.sharding import PartitionSpec as P

EPSILON = 1e-05


def side_by_side(arrays, axis, split_dim, concat_dim, along):
    widths = [a.shape[along] for a in arrays]
    both = jnp.concatenate(arrays, axis=along)
    filled = lax.all_to_all(both, axis, split_axis=split_dim, concat_axis=concat_dim, tiled=True)
    return tuple(jnp.split(filled, [sum(widths[:k]) for k in range(1, len(widths))], axis=along))


def together(arrays, axis):
    vector, at, outs = (jnp.concatenate([a.reshape(-1) for a in arrays]), 0, [])
    total = lax.psum(vector, axis)
    for a in arrays:
        outs.append(total[at : at + a.size].reshape(a.shape))
        at += a.size
    return tuple(outs)


def for_sending(x):
    return jax.tree.map(lambda a: a.astype(jnp.bfloat16) if a.dtype == jnp.float32 else a, x)


def contract(pattern, left_side, right_side):
    return jnp.einsum(pattern, left_side, right_side, preferred_element_type=jnp.float32)


def norm_forward(values, gain_vec, bias_vec, norm_axis):
    center = values - jnp.mean(values, axis=norm_axis, keepdims=True)
    inv_std = lax.rsqrt(jnp.mean(center * center, axis=norm_axis, keepdims=True) + EPSILON)
    normed = center * inv_std
    return (normed, inv_std, normed * gain_vec + bias_vec)


def norm_backward(upstream, normed, inv_std, gain_vec, norm_axis, others):
    grad_gain = jnp.sum(upstream * normed, axis=others)
    grad_bias = jnp.sum(upstream, axis=others)
    scaled = upstream * gain_vec
    result = inv_std * (
        scaled
        - jnp.mean(scaled, axis=norm_axis, keepdims=True)
        - normed * jnp.mean(scaled * normed, axis=norm_axis, keepdims=True)
    )
    return (result, grad_gain, grad_bias)


def enter_rows(pair_rows, row_keep, col_keep, proj_weight, norm_gain, norm_bias):
    channels = pair_rows.shape[2]
    normed_in, inv_in, scaled_in = norm_forward(
        pair_rows.astype(jnp.float32), norm_gain[0], norm_bias[0], 2
    )
    input_bf = scaled_in.astype(jnp.bfloat16)
    factor_pre = contract("rld,de->erl", input_bf, proj_weight[:, : 4 * channels])
    gate_pre = contract("rld,de->rle", input_bf, proj_weight[:, 4 * channels :])
    keep_both = row_keep[:, None] * col_keep[None, :]
    left_bf = (
        jax.nn.sigmoid(factor_pre[:channels]) * factor_pre[channels : 2 * channels] * keep_both
    ).astype(jnp.bfloat16)
    right_bf = (
        jax.nn.sigmoid(factor_pre[2 * channels : 3 * channels])
        * factor_pre[3 * channels :]
        * keep_both
    ).astype(jnp.bfloat16)
    return (input_bf, normed_in, inv_in, factor_pre, gate_pre, keep_both, left_bf, right_bf)


def middle_rows(
    pair_rows,
    cot_rows,
    product_bf,
    gate_pre,
    out_weight,
    up_weight,
    down_weight,
    norm_gain,
    norm_bias,
):
    prod_normed, prod_inv, prod_scaled = norm_forward(
        product_bf.astype(jnp.float32), norm_gain[1][:, None, None], norm_bias[1][:, None, None], 0
    )
    prod_norm_bf = prod_scaled.astype(jnp.bfloat16)
    update = contract("crj,cd->rjd", prod_norm_bf, out_weight)
    gate_sig = jax.nn.sigmoid(gate_pre)
    first_bf = (pair_rows.astype(jnp.float32) + gate_sig * update).astype(jnp.bfloat16)
    tran_normed, tran_inv, tran_scaled = norm_forward(
        first_bf.astype(jnp.float32), norm_gain[2], norm_bias[2], 2
    )
    tran_bf = tran_scaled.astype(jnp.bfloat16)
    hidden_pre = contract("rld,dh->rlh", tran_bf, up_weight)
    hidden_sig = jax.nn.sigmoid(hidden_pre)
    hidden_bf = (hidden_pre * hidden_sig).astype(jnp.bfloat16)
    grad_down = contract("rlh,rld->hd", hidden_bf, cot_rows)
    hidden_grad_bf = (
        contract("rld,hd->rlh", cot_rows, down_weight)
        * hidden_sig
        * (1.0 + hidden_pre * (1.0 - hidden_sig))
    ).astype(jnp.bfloat16)
    grad_up = contract("rld,rlh->dh", tran_bf, hidden_grad_bf)
    tran_grad = contract("rlh,dh->rld", hidden_grad_bf, up_weight)
    first_grad, gain_tran, bias_tran = norm_backward(
        tran_grad, tran_normed, tran_inv, norm_gain[2], 2, (0, 1)
    )
    first_grad = first_grad + cot_rows.astype(jnp.float32)
    update_grad_bf = (first_grad * gate_sig).astype(jnp.bfloat16)
    gate_grad_bf = (first_grad * update * gate_sig * (1.0 - gate_sig)).astype(jnp.bfloat16)
    grad_out = contract("crj,rjd->cd", prod_norm_bf, update_grad_bf)
    norm_grad = contract("rjd,cd->crj", update_grad_bf, out_weight)
    prod_grad, gain_prod, bias_prod = norm_backward(
        norm_grad, prod_normed, prod_inv, norm_gain[1][:, None, None], 0, (1, 2)
    )
    return (
        prod_grad.astype(jnp.bfloat16),
        first_grad,
        gate_grad_bf,
        grad_out,
        grad_up,
        grad_down,
        gain_prod,
        bias_prod,
        gain_tran,
        bias_tran,
    )


def leave_rows(
    left_grad,
    right_grad,
    factor_pre,
    keep_both,
    gate_grad_bf,
    input_bf,
    normed_in,
    inv_in,
    first_grad,
    proj_weight,
    norm_gain,
):
    channels = gate_grad_bf.shape[2]
    sig_left = jax.nn.sigmoid(factor_pre[:channels])
    lin_left = factor_pre[channels : 2 * channels]
    sig_right = jax.nn.sigmoid(factor_pre[2 * channels : 3 * channels])
    lin_right = factor_pre[3 * channels :]
    masked_left = left_grad.astype(jnp.float32) * keep_both
    masked_right = right_grad.astype(jnp.float32) * keep_both
    factor_grad = jnp.concatenate(
        [
            masked_left * lin_left * sig_left * (1.0 - sig_left),
            masked_left * sig_left,
            masked_right * lin_right * sig_right * (1.0 - sig_right),
            masked_right * sig_right,
        ],
        axis=0,
    ).astype(jnp.bfloat16)
    grad_proj = jnp.concatenate(
        [
            contract("rld,erl->de", input_bf, factor_grad),
            contract("rld,rle->de", input_bf, gate_grad_bf),
        ],
        axis=1,
    )
    input_grad = contract("erl,de->rld", factor_grad, proj_weight[:, : 4 * channels]) + contract(
        "rle,de->rld", gate_grad_bf, proj_weight[:, 4 * channels :]
    )
    pair_grad, gain_in, bias_in = norm_backward(
        input_grad, normed_in, inv_in, norm_gain[0], 2, (0, 1)
    )
    return ((pair_grad + first_grad).astype(jnp.bfloat16), grad_proj, gain_in, bias_in)


def channel_products(left_part, right_part):
    return contract("acik,acjk->acij", left_part, right_part).astype(jnp.bfloat16)


def channel_grads(grad_part, left_part, right_part):
    left_grad = contract("acij,acjk->acik", grad_part, right_part).astype(jnp.bfloat16)
    right_grad = contract("acij,acik->acjk", grad_part, left_part).astype(jnp.bfloat16)
    return (left_grad, right_grad)


def local(
    pair, cotangent, lengths, proj_weight, out_weight, up_weight, down_weight, norm_gain, norm_bias
):
    pair_rows = pair[0]
    cot_rows = cotangent[0]
    rows_here, length_all, channels = pair_rows.shape
    groups = lax.axis_size("row")
    per_group = channels // groups
    first_row = lax.axis_index("row") * rows_here
    row_keep = (first_row + jnp.arange(rows_here, dtype=jnp.int32) < lengths[0]).astype(jnp.float32)
    col_keep = (jnp.arange(length_all, dtype=jnp.int32) < lengths[0]).astype(jnp.float32)
    entered = enter_rows(pair_rows, row_keep, col_keep, proj_weight, norm_gain, norm_bias)
    input_bf, normed_in, inv_in, factor_pre, gate_pre, keep_both, left_bf, right_bf = entered
    left_split = left_bf.reshape(groups, per_group, rows_here, length_all)
    right_split = right_bf.reshape(groups, per_group, rows_here, length_all)
    left_owned, right_owned = side_by_side((left_split, right_split), "row", 0, 2, 1)
    product_owned = channel_products(left_owned, right_owned)
    product_split = lax.all_to_all(product_owned, "row", split_axis=2, concat_axis=0, tiled=True)
    product_bf = product_split.reshape(channels, rows_here, length_all)
    middle = middle_rows(
        pair_rows,
        cot_rows,
        product_bf,
        gate_pre,
        out_weight,
        up_weight,
        down_weight,
        norm_gain,
        norm_bias,
    )
    (
        prod_grad_bf,
        first_grad,
        gate_grad_bf,
        grad_out,
        grad_up,
        grad_down,
        gain_prod,
        bias_prod,
        gain_tran,
        bias_tran,
    ) = middle
    summed_up, summed_down = together((grad_up, grad_down), ("crop", "row"))
    grad_split = prod_grad_bf.reshape(groups, per_group, rows_here, length_all)
    grad_owned = lax.all_to_all(grad_split, "row", split_axis=0, concat_axis=2, tiled=True)
    left_home, right_home = lax.all_to_all(
        for_sending(channel_grads(grad_owned, left_owned, right_owned)),
        "row",
        split_axis=2,
        concat_axis=0,
        tiled=True,
    )
    left_grad = left_home.reshape(channels, rows_here, length_all)
    right_grad = right_home.reshape(channels, rows_here, length_all)
    pair_grad, grad_proj, gain_in, bias_in = leave_rows(
        left_grad,
        right_grad,
        factor_pre,
        keep_both,
        gate_grad_bf,
        input_bf,
        normed_in,
        inv_in,
        first_grad,
        proj_weight,
        norm_gain,
    )
    gain_all = jnp.stack([gain_in, gain_prod, gain_tran])
    bias_all = jnp.stack([bias_in, bias_prod, bias_tran])
    summed_proj, summed_out, summed_gain, summed_bias = lax.psum(
        (grad_proj, grad_out, gain_all, bias_all), ("crop", "row")
    )
    factor = 1.0 / (rows_here * groups)
    return (
        pair_grad[None],
        summed_proj * factor,
        summed_out * factor,
        summed_up * factor,
        summed_down * factor,
        summed_gain * factor,
        summed_bias * factor,
    )


def solution(mesh):
    in_specs = (
        P("crop", "row", None, None),
        P("crop", "row", None, None),
        P("crop"),
        P(),
        P(),
        P(),
        P(),
        P(),
        P(),
    )
    out_specs = (P("crop", "row", None, None), P(), P(), P(), P(), P(), P())
    return jax.shard_map(local, mesh=mesh, in_specs=in_specs, out_specs=out_specs, check_vma=False)
```

profile of v0, /device:TPU:1, one launch (start us, length us, event | category | flops | bytes accessed | tf_op | source)
XLA Modules:
  0.0 556.9 jit_solution(11000184731263995300)
XLA Ops:
  17.9 3.2 pad_maximum_fusion.1
  22.3 62.7 %all_to_all.60 = bf16[64,4,8,512]{3,1,2,0:T(4,128)(2,1)S(1)} all-to-all(bf16[64,4,8,512]{3,1,2,0:T(4,128)(2,1)S(1)} %copy.100), channel_id=1, replica_groups=mesh['crop'=4,'row'=64] {'row'}, dimensions={0} | all-to-all | bytes 4194304 | tf_op jit(solution)/shard_map/all_to_all | solution.py:12
  89.7 5.6 all-to-all-start.1
  96.6 27.0 %all-to-all-done.1 = bf16[1,2,512,512]{3,1,0,2:T(2,128)(2,1)S(1)} async-done(((bf16[1,2,512,512]{3,1,0,2:T(2,128)(2,1)}), bf16[1,2,512,512]{3,1,0,2:T(2,128)(2,1)S(1)}, u32[]{:S(2)}, u32[]{:S(2)}) %all-to-all-start.1) | async-done | bytes 1048608 | tf_op jit(solution)/shard_map/all_to_all | solution.py:202
  128.0 2.7 reshape.204
  132.1 2.5 convert_reduce_fusion
  137.0 3.4 multiply_convert_fusion.1
  140.5 3.2 fusion.81
  145.9 2.8 fusion.20
  148.8 4.7 multiply_convert_fusion.3
  157.9 2.3 reshape.200
  160.2 3.4 copy.62
  163.5 5.5 all-to-all-start.2
  169.1 3.3 convolution_bitcast_fusion.2
  172.4 2.4 reduce_sum.178
  174.8 22.4 %all-to-all-done.2 = bf16[64,2,8,512]{3,1,2,0:T(2,128)(2,1)} async-done(((bf16[64,2,8,512]{3,1,2,0:T(2,128)(2,1)}), bf16[64,2,8,512]{3,1,2,0:T(2,128)(2,1)}, u32[]{:S(2)}, u32[]{:S(2)}) %all-to-all-start.2) | async-done | bytes 1048608 | tf_op jit(solution)/shard_map/all_to_all | solution.py:229
  201.5 6.1 %all-to-all-start.3 = ((bf16[1,2,512,512]{3,1,0,2:T(2,128)(2,1)}), bf16[1,2,512,512]{3,1,0,2:T(2,128)(2,1)}, u32[]{:S(2)}, u32[]{:S(2)}) async-start(bf16[1,2,512,512]{3,1,0,2:T(2,128)(2,1)} %copy.64), calls=%async_computation.3 | async-start | bytes 2097152 | tf_op jit(solution)/shard_map/all_to_all | solution.py:230
  207.6 2.7 convolution_bitcast_fusion.4
  211.5 6.6 %convolution_bitcast_fusion = f32[65536]{0:T(1024)} fusion(f32[8,512,512]{2,1,0:T(8,128)} %copy-done.11, bf16[1,8,512,128]{3,2,1,0:T(8,128)(2,1)S(1)} %copy-done.21), kind=kOutput, calls=%fused_computation | convolution fusion | flops 547356672 | bytes 9699328 | tf_op jit(solution)/shard_map/rlh,rld->hd/dot_general | solution.py:30
  222.3 13.3 %all-to-all-done.3 = bf16[1,2,512,512]{3,1,0,2:T(2,128)(2,1)} async-done(((bf16[1,2,512,512]{3,1,0,2:T(2,128)(2,1)}), bf16[1,2,512,512]{3,1,0,2:T(2,128)(2,1)}, u32[]{:S(2)}, u32[]{:S(2)}) %all-to-all-start.3) | async-done | bytes 1048608 | tf_op jit(solution)/shard_map/all_to_all | solution.py:230
  235.6 5.5 all-to-all-start.4
  243.0 3.3 copy_bitcast_fusion.1
  246.3 3.8 reshape.205
  250.1 19.1 %all-to-all-done.4 = bf16[1,2,512,512]{3,1,0,2:T(2,128)(2,1)} async-done(((bf16[1,2,512,512]{3,1,0,2:T(2,128)(2,1)}), bf16[1,2,512,512]{3,1,0,2:T(2,128)(2,1)}, u32[]{:S(2)}, u32[]{:S(2)}) %all-to-all-start.4) | async-done | bytes 1048608 | tf_op jit(solution)/shard_map/all_to_all | solution.py:230
  269.1 3.3 copy_bitcast_fusion
  272.4 3.7 reshape.206
  276.1 5.6 %multiply_convert_fusion.7 = (bf16[128,8,512]{2,0,1:T(8,128)(2,1)S(1)}, bf16[128,8,512]{2,0,1:T(8,128)(2,1)S(1)}, bf16[128,8,512]{2,0,1:T(8,128)(2,1)S(1)}, bf16[128,8,512]{2,0,1:T(8,128)(2,1)S(1)}) fusion(f32[512,8,512]{2,0,1:T(8,128)} %copy-done.2, f32[128,8,512]{2,0,1:T(8,128)} %reshape.205, f32[8,512]{1,0:T(8,128)S(1)} %copy-done.31, ...), kind=kLoop, calls=%fused_computation.62 | loop fusion | flops 11534336 | bytes 16793600 | tf_op jit(solution)/shard_map/convert.11
  284.6 2.8 fusion.29
  288.9 4.7 fusion.47
  293.7 2.3 copy.81
  296.0 75.2 %all-reduce = (f32[3,128]{1,0:T(4,128)S(1)}, f32[3,128]{1,0:T(4,128)S(1)}) all-reduce(f32[3,128]{1,0:T(4,128)S(1)} %pad_maximum_fusion.6, f32[3,128]{1,0:T(4,128)S(1)} %pad_maximum_fusion.7), channel_id=1, replica_groups=mesh['crop'=4,'row'=64] {'crop','row'}, use_global_device_ids=true, to_apply=%region_18.0 | all-reduce | flops 768 | bytes 6144 | tf_op jit(solution)/shard_map/psum | solution.py:254
  372.3 171.8 %all-reduce.4.cloned.1.call-done = (f32[128,640]{1,0:T(8,128)}, f32[128,128]{1,0:T(8,128)}, f32[131072]{0:T(1024)}) async-done(((f32[128,640]{1,0:T(8,128)}, f32[128,128]{1,0:T(8,128)}, f32[131072]{0:T(1024)}), (f32[128,640]{1,0:T(8,128)}, f32[128,128]{1,0:T(8,128)}, f32[131072]{0:T(1024)})) %all-reduce.4.cloned.1.call-update) | async-done | bytes 917520 | tf_op jit(solution)/shard_map/psum | solution.py:254
  (158 shorter events, 54.3 us)
Async XLA Ops:
  7.2 128.4 %copy-start = (bf16[128,512]{1,0:T(8,128)(2,1)S(1)}, bf16[128,512]{1,0:T(8,128)(2,1)}, u32[]{:S(2)}) copy-start(bf16[128,512]{1,0:T(8,128)(2,1)} %param.14) | copy-start | bytes 393220
  9.6 122.3 %copy-start.22 = (f32[8,512]{1,0:T(8,128)}, f32[8,512]{1,0:T(8,128)S(1)}, u32[]{:S(2)}) copy-start(f32[8,512]{1,0:T(8,128)S(1)} %broadcast_multiply_fusion.11) | copy-start | bytes 49156
  10.0 122.0 %copy-start.26 = (f32[8,512]{1,0:T(8,128)}, f32[8,512]{1,0:T(8,128)S(1)}, u32[]{:S(2)}) copy-start(f32[8,512]{1,0:T(8,128)S(1)} %add_rsqrt_fusion.2) | copy-start | bytes 49156
  10.5 120.2 %copy-start.38 = (f32[128]{0:T(128)}, f32[128]{0:T(128)S(1)}, u32[]{:S(2)}) copy-start(f32[128]{0:T(128)S(1)} %get-tuple-element.61) | copy-start | bytes 1540
  10.5 121.5 %copy-start.36 = (f32[128]{0:T(128)}, f32[128]{0:T(128)S(1)}, u32[]{:S(2)}) copy-start(f32[128]{0:T(128)S(1)} %get-tuple-element.62) | copy-start | bytes 1540
  10.5 121.5 %copy-start.40 = (f32[128]{0:T(128)}, f32[128]{0:T(128)S(1)}, u32[]{:S(2)}) copy-start(f32[128]{0:T(128)S(1)} %get-tuple-element.54) | copy-start | bytes 1540
  12.0 3.2 copy-start.2
  87.5 7.7 %copy-start.19 = (bf16[1,8,512,128]{3,2,1,0:T(8,128)(2,1)S(1)}, bf16[1,8,512,128]{3,2,1,0:T(8,128)(2,1)}, u32[]{:S(2)}) copy-start(bf16[1,8,512,128]{3,2,1,0:T(8,128)(2,1)} %param.10) | copy-start | bytes 3145732
  89.7 33.9 %all-to-all-start.1 = ((bf16[1,2,512,512]{3,1,0,2:T(2,128)(2,1)}), bf16[1,2,512,512]{3,1,0,2:T(2,128)(2,1)S(1)}, u32[]{:S(2)}, u32[]{:S(2)}) async-start(bf16[1,2,512,512]{3,1,0,2:T(2,128)(2,1)} %copy.52), calls=%async_computation.1 | async-start | bytes 2097152 | tf_op jit(solution)/shard_map/all_to_all | solution.py:202
  132.0 3.5 copy-start.34
  132.1 3.5 copy-start.43
  134.9 34.1 %copy-start.24 = (f32[8,512]{1,0:T(8,128)}, f32[8,512]{1,0:T(8,128)S(1)}, u32[]{:S(2)}) copy-start(f32[8,512]{1,0:T(8,128)S(1)} %add_rsqrt_fusion) | copy-start | bytes 49156
  137.0 3.5 copy-start.11
  140.5 3.2 copy-start.13
  148.7 4.7 copy-start.4
  148.8 4.7 copy-start.39
  160.2 8.9 %copy-start.44 = (f32[128]{0:T(128)S(1)}, f32[128]{0:T(128)}, u32[]{:S(2)}) copy-start(f32[128]{0:T(128)} %get-tuple-element.53) | copy-start | bytes 1540
  163.5 33.6 %all-to-all-start.2 = ((bf16[64,2,8,512]{3,1,2,0:T(2,128)(2,1)}), bf16[64,2,8,512]{3,1,2,0:T(2,128)(2,1)}, u32[]{:S(2)}, u32[]{:S(2)}) async-start(bf16[64,2,8,512]{3,1,2,0:T(2,128)(2,1)} %copy.62), calls=%async_computation.2 | async-start | bytes 2097152 | tf_op jit(solution)/shard_map/all_to_all | solution.py:229
  201.5 8.8 %copy-start.23 = (f32[8,512]{1,0:T(8,128)S(1)}, f32[8,512]{1,0:T(8,128)}, u32[]{:S(2)}) copy-start(f32[8,512]{1,0:T(8,128)} %copy-done.22) | copy-start | bytes 49156
  201.5 8.8 %copy-start.27 = (f32[8,512]{1,0:T(8,128)S(1)}, f32[8,512]{1,0:T(8,128)}, u32[]{:S(2)}) copy-start(f32[8,512]{1,0:T(8,128)} %copy-done.26) | copy-start | bytes 49156
  201.5 8.8 %copy-start.37 = (f32[128]{0:T(128)S(1)}, f32[128]{0:T(128)}, u32[]{:S(2)}) copy-start(f32[128]{0:T(128)} %copy-done.36) | copy-start | bytes 1540
  201.5 8.8 %copy-start.41 = (f32[128]{0:T(128)S(1)}, f32[128]{0:T(128)}, u32[]{:S(2)}) copy-start(f32[128]{0:T(128)} %copy-done.40) | copy-start | bytes 1540
  201.5 34.1 %all-to-all-start.3 = ((bf16[1,2,512,512]{3,1,0,2:T(2,128)(2,1)}), bf16[1,2,512,512]{3,1,0,2:T(2,128)(2,1)}, u32[]{:S(2)}, u32[]{:S(2)}) async-start(bf16[1,2,512,512]{3,1,0,2:T(2,128)(2,1)} %copy.64), calls=%async_computation.3 | async-start | bytes 2097152 | tf_op jit(solution)/shard_map/all_to_all | solution.py:230
  211.5 6.6 %copy-start.18 = (bf16[1,4,64,8,512]{4,3,2,1,0:T(8,128)(2,1)S(1)}, bf16[1,4,64,8,512]{4,3,2,1,0:T(8,128)(2,1)}, u32[]{:S(2)}) copy-start(bf16[1,4,64,8,512]{4,3,2,1,0:T(8,128)(2,1)} %copy-done.17) | copy-start | bytes 6291460
  235.6 33.5 %all-to-all-start.4 = ((bf16[1,2,512,512]{3,1,0,2:T(2,128)(2,1)}), bf16[1,2,512,512]{3,1,0,2:T(2,128)(2,1)}, u32[]{:S(2)}, u32[]{:S(2)}) async-start(bf16[1,2,512,512]{3,1,0,2:T(2,128)(2,1)} %copy.67), calls=%async_computation.4 | async-start | bytes 2097152 | tf_op jit(solution)/shard_map/all_to_all | solution.py:230
  241.1 303.0 %all-reduce.4.cloned.1.call-start = ((), (), s32[]{:S(2)}) async-start(), calls=%async_computation.5 | async-start | bytes 1835008 | tf_op jit(solution)/shard_map/psum | solution.py:254
  272.4 3.7 copy-start.31
  284.6 4.3 copy-start.25
  288.9 4.8 copy-start.42
  288.9 4.7 copy-start.45
  288.9 4.7 copy-start.46
  293.7 256.2 %copy-start.1 = (bf16[128,512]{1,0:T(8,128)(2,1)S(1)}, bf16[128,512]{1,0:T(8,128)(2,1)}, u32[]{:S(2)}) copy-start(bf16[128,512]{1,0:T(8,128)(2,1)} %param.14) | copy-start | bytes 393220
  (23 other events, 43.0 us)
Sparse Core Ops, SparseCore 0:
  288.3 255.7 all-reduce.3
where the time goes:
time: 565 us; the launch traced here: 557 us
  waiting for transfers between devices  254 us (45%)
  blocking collectives  138 us (24%)
  other arithmetic  48.3 us (9%)
  local copies, waits for them, and re-layouts  41.2 us (7%)
  matrix products  37.6 us (7%)
  starting transfers between devices  22.7 us (4%)
  between operations  15.6 us (3%)
    psum x1, waiting for transfers between devices, local(): lax.psum((grad_proj, grad_out, gain_all, bias_all), ('crop', 'row'))  172 us
    psum x1, blocking collectives, local(): lax.psum((grad_proj, grad_out, gain_all, bias_all), ('crop', 'row'))  75.2 us
    all_to_all x1, blocking collectives, side_by_side(): lax.all_to_all(both, axis, split_axis=split_dim, concat_axis=concat_dim,...  62.7 us
    dot_general x17, matrix products, contract(): jnp.einsum(pattern, left_side, right_side, preferred_element_type=jnp.flo...  37.6 us
    all_to_all x2, waiting for transfers between devices, local(): lax.all_to_all(for_sending(channel_grads(grad_owned, left_owned, right_ow...  32.4 us
    all_to_all x1, waiting for transfers between devices, local(): lax.all_to_all(product_owned, 'row', split_axis=2, concat_axis=0, tiled=T...  27 us
    all_to_all x1, waiting for transfers between devices, local(): lax.all_to_all(grad_split, 'row', split_axis=0, concat_axis=2, tiled=True)  22.4 us
    all_to_all x2, starting transfers between devices, local(): lax.all_to_all(for_sending(channel_grads(grad_owned, left_owned, right_ow...  11.6 us
  transfers between devices with their start and end apart: 5, of which 5 were waited for; matrix products, arithmetic and copies ran while one was open for 7% of the time, Pallas kernels for 0%

commit v1 on v0

--- a/solution.py
+++ b/solution.py
@@ -4,6 +4,11 @@
 from jax.sharding import PartitionSpec as P
 
 EPSILON = 1e-05
+
+
+def list_quotas(frame):
+    w1 = jax.lax.psum(frame, "row")
+    return jax.lax.psum(w1, "crop")
 
 
 def side_by_side(arrays, axis, split_dim, concat_dim, along):
@@ -251,8 +256,8 @@
     )
     gain_all = jnp.stack([gain_in, gain_prod, gain_tran])
     bias_all = jnp.stack([bias_in, bias_prod, bias_tran])
-    summed_proj, summed_out, summed_gain, summed_bias = lax.psum(
-        (grad_proj, grad_out, gain_all, bias_all), ("crop", "row")
+    summed_proj, summed_out, summed_gain, summed_bias = list_quotas(
+        (grad_proj, grad_out, gain_all, bias_all)
     )
     factor = 1.0 / (rows_here * groups)
     return (

time: 565 us -> 1300 us (2.30)
  waiting for transfers between devices: 254 us -> 834 us
  blocking collectives: 138 us -> 294 us
    psum x1 -> x3, waiting for transfers between devices: 172 us -> 792 us  [the longest x1 446 us: list_quotas(): w1 = jax.lax.psum(frame, 'row')]
    psum x1 -> x2, blocking collectives: 75.2 us -> 198 us  [the longest x1 164 us: list_quotas(): w1 = jax.lax.psum(frame, 'row')]
    all_to_all x0 -> x1, blocking collectives: none -> 33.1 us  [local(): lax.all_to_all(grad_split, 'row', split_axis=0, concat_axis=2, tiled=True)]
    all_to_all x1 -> x0, waiting for transfers between devices: 22.4 us -> none  [local(): lax.all_to_all(grad_split, 'row', split_axis=0, concat_axis=2, tiled=True)]
    all_to_all x2, waiting for transfers between devices: 32.4 us -> 15.1 us  [local(): lax.all_to_all(for_sending(channel_grads(grad_owned, left_owned, right_ow...]
  transfers between devices with their start and end apart: 5 -> 6, of which waited for: 5 -> 5; matrix products, arithmetic and copies ran while one was open for 7% -> 3% of each run, Pallas kernels for 0% -> 0%
where the time goes in v1:
time: 1300 us; the launch traced here: 1290 us
  waiting for transfers between devices  834 us (64%)
  blocking collectives  294 us (23%)
  other arithmetic  47.7 us (4%)
  local copies, waits for them, and re-layouts  41.3 us (3%)
  matrix products  35.5 us (3%)
  between operations  17.5 us (1%)
  starting transfers between devices  17 us (1%)
    psum x1, waiting for transfers between devices, list_quotas(): w1 = jax.lax.psum(frame, 'row')  446 us
    psum x1, waiting for transfers between devices, together(): total = lax.psum(vector, axis)  254 us
    psum x1, blocking collectives, list_quotas(): w1 = jax.lax.psum(frame, 'row')  164 us
    psum x1, waiting for transfers between devices, list_quotas(): return jax.lax.psum(w1, 'crop')  92.7 us
    all_to_all x1, blocking collectives, side_by_side(): lax.all_to_all(both, axis, split_axis=split_dim, concat_axis=concat_dim,...  62.7 us
    dot_general x17, matrix products, contract(): jnp.einsum(pattern, left_side, right_side, preferred_element_type=jnp.flo...  35.5 us
    psum x1, blocking collectives, list_quotas(): return jax.lax.psum(w1, 'crop')  34.1 us
    all_to_all x1, blocking collectives, local(): lax.all_to_all(grad_split, 'row', split_axis=0, concat_axis=2, tiled=True)  33.1 us
  transfers between devices with their start and end apart: 6, of which 5 were waited for; matrix products, arithmetic and copies ran while one was open for 3% of the time, Pallas kernels for 0%

profile of v1, /device:TPU:1, one launch (start us, length us, event | category | flops | bytes accessed | tf_op | source)
XLA Modules:
  0.0 1287.4 jit_solution(14658209645718938657)
XLA Ops:
  18.8 3.2 pad_maximum_fusion.1
  23.2 62.7 %all_to_all.60 = bf16[64,4,8,512]{3,1,2,0:T(4,128)(2,1)S(1)} all-to-all(bf16[64,4,8,512]{3,1,2,0:T(4,128)(2,1)S(1)} %copy.100), channel_id=1, replica_groups=mesh['crop'=4,'row'=64] {'row'}, dimensions={0} | all-to-all | bytes 4194304 | tf_op jit(solution)/shard_map/all_to_all | solution.py:17
  90.5 5.6 all-to-all-start.1
  97.4 27.0 %all-to-all-done.1 = bf16[1,2,512,512]{3,1,0,2:T(2,128)(2,1)S(1)} async-done(((bf16[1,2,512,512]{3,1,0,2:T(2,128)(2,1)}), bf16[1,2,512,512]{3,1,0,2:T(2,128)(2,1)S(1)}, u32[]{:S(2)}, u32[]{:S(2)}) %all-to-all-start.1) | async-done | bytes 1048608 | tf_op jit(solution)/shard_map/all_to_all | solution.py:207
  128.8 2.7 reshape.204
  132.9 2.6 convert_reduce_fusion
  137.9 3.4 multiply_convert_fusion.1
  141.4 3.1 fusion.81
  146.7 2.8 fusion.20
  149.6 4.7 multiply_convert_fusion.3
  158.9 2.3 reshape.200
  161.1 2.5 copy.62
  163.7 33.1 %all_to_all.61 = bf16[64,2,8,512]{3,1,2,0:T(2,128)(2,1)S(1)} all-to-all(bf16[64,2,8,512]{3,1,2,0:T(2,128)(2,1)S(1)} %copy.62), channel_id=1, replica_groups=mesh['crop'=4,'row'=64] {'row'}, dimensions={0} | all-to-all | bytes 2097152 | tf_op jit(solution)/shard_map/all_to_all | solution.py:234
  200.5 5.8 all-to-all-start.3
  206.4 3.4 convolution_bitcast_fusion.2
  209.8 6.6 convolution_bitcast_fusion
  219.3 15.1 %all-to-all-done.3 = bf16[1,2,512,512]{3,1,0,2:T(2,128)(2,1)} async-done(((bf16[1,2,512,512]{3,1,0,2:T(2,128)(2,1)}), bf16[1,2,512,512]{3,1,0,2:T(2,128)(2,1)}, u32[]{:S(2)}, u32[]{:S(2)}) %all-to-all-start.3) | async-done | bytes 1048608 | tf_op jit(solution)/shard_map/all_to_all | solution.py:235
  234.4 5.5 all-to-all-start.4
  241.9 2.6 convolution_bitcast_fusion.4
  244.5 2.4 reduce_sum.178
  248.6 253.6 %all-reduce.8.cloned.1.call-done = f32[131072]{0:T(1024)} async-done(((f32[131072]{0:T(1024)}), f32[131072]{0:T(1024)}) %all-reduce.8.cloned.1.call-update) | async-done | bytes 524304 | tf_op jit(solution)/shard_map/psum | solution.py:23
  504.7 3.3 copy_bitcast_fusion.1
  508.1 3.9 reshape.205
  512.0 3.3 copy_bitcast_fusion
  515.3 3.7 reshape.206
  519.0 5.6 multiply_convert_fusion.7
  527.5 2.8 fusion.29
  531.2 4.8 fusion.47
  538.3 164.1 %all-reduce = (f32[3,128]{1,0:T(4,128)S(1)}, f32[3,128]{1,0:T(4,128)S(1)}) all-reduce(f32[3,128]{1,0:T(4,128)S(1)} %pad_maximum_fusion.6, f32[3,128]{1,0:T(4,128)S(1)} %pad_maximum_fusion.7), channel_id=1, replica_groups=mesh['crop'=4,'row'=64] {'row'}, use_global_device_ids=true, to_apply=%region_20.0 | all-reduce | flops 768 | bytes 6144 | tf_op jit(solution)/shard_map/psum | solution.py:10
  702.5 34.1 %all-reduce.2 = (f32[3,128]{1,0:T(4,128)S(1)}, f32[3,128]{1,0:T(4,128)S(1)}) all-reduce(f32[3,128]{1,0:T(4,128)S(1)} %get-tuple-element.31, f32[3,128]{1,0:T(4,128)S(1)} %get-tuple-element.32), channel_id=1, replica_groups=mesh['crop'=4,'row'=64] {'crop'}, use_global_device_ids=true, to_apply=%region_21.0 | all-reduce | flops 768 | bytes 6144 | tf_op jit(solution)/shard_map/psum | solution.py:11
  736.6 445.7 %all-reduce.10.cloned.1.call-done = (f32[128,640]{1,0:T(8,128)}, f32[128,128]{1,0:T(8,128)}) async-done(((f32[128,640]{1,0:T(8,128)}, f32[128,128]{1,0:T(8,128)}), (f32[128,640]{1,0:T(8,128)}, f32[128,128]{1,0:T(8,128)})) %all-reduce.10.cloned.1.call-update) | async-done | bytes 393232 | tf_op jit(solution)/shard_map/psum | solution.py:10
  1183.5 92.7 %all-reduce.12.cloned.1.call-done = (f32[128,640]{1,0:T(8,128)}, f32[128,128]{1,0:T(8,128)}) async-done(((f32[128,640]{1,0:T(8,128)}, f32[128,128]{1,0:T(8,128)}), (f32[128,640]{1,0:T(8,128)}, f32[128,128]{1,0:T(8,128)})) %all-reduce.12.cloned.1.call-update) | async-done | bytes 393232 | tf_op jit(solution)/shard_map/psum | solution.py:11
  (186 shorter events, 55.0 us)
Async XLA Ops:
  8.0 128.5 %copy-start = (bf16[128,512]{1,0:T(8,128)(2,1)S(1)}, bf16[128,512]{1,0:T(8,128)(2,1)}, u32[]{:S(2)}) copy-start(bf16[128,512]{1,0:T(8,128)(2,1)} %param.14) | copy-start | bytes 393220
  10.5 122.4 %copy-start.24 = (f32[8,512]{1,0:T(8,128)}, f32[8,512]{1,0:T(8,128)S(1)}, u32[]{:S(2)}) copy-start(f32[8,512]{1,0:T(8,128)S(1)} %broadcast_multiply_fusion.11) | copy-start | bytes 49156
  10.8 122.0 %copy-start.29 = (f32[8,512]{1,0:T(8,128)}, f32[8,512]{1,0:T(8,128)S(1)}, u32[]{:S(2)}) copy-start(f32[8,512]{1,0:T(8,128)S(1)} %add_rsqrt_fusion.2) | copy-start | bytes 49156
  11.4 120.2 %copy-start.46 = (f32[128]{0:T(128)}, f32[128]{0:T(128)S(1)}, u32[]{:S(2)}) copy-start(f32[128]{0:T(128)S(1)} %get-tuple-element.64) | copy-start | bytes 1540
  11.4 121.5 %copy-start.43 = (f32[128]{0:T(128)}, f32[128]{0:T(128)S(1)}, u32[]{:S(2)}) copy-start(f32[128]{0:T(128)S(1)} %get-tuple-element.65) | copy-start | bytes 1540
  11.4 121.5 %copy-start.48 = (f32[128]{0:T(128)}, f32[128]{0:T(128)S(1)}, u32[]{:S(2)}) copy-start(f32[128]{0:T(128)S(1)} %get-tuple-element.57) | copy-start | bytes 1540
  88.4 7.7 copy-start.19
  90.5 33.9 %all-to-all-start.1 = ((bf16[1,2,512,512]{3,1,0,2:T(2,128)(2,1)}), bf16[1,2,512,512]{3,1,0,2:T(2,128)(2,1)S(1)}, u32[]{:S(2)}, u32[]{:S(2)}) async-start(bf16[1,2,512,512]{3,1,0,2:T(2,128)(2,1)} %copy.52), calls=%async_computation.1 | async-start | bytes 2097152 | tf_op jit(solution)/shard_map/all_to_all | solution.py:207
  135.8 70.5 %copy-start.27 = (f32[8,512]{1,0:T(8,128)}, f32[8,512]{1,0:T(8,128)S(1)}, u32[]{:S(2)}) copy-start(f32[8,512]{1,0:T(8,128)S(1)} %add_rsqrt_fusion) | copy-start | bytes 49156
  149.5 4.7 copy-start.36
  149.5 4.7 copy-start.38
  149.5 4.7 copy-start.4
  149.5 4.7 copy-start.47
  161.1 36.6 %copy-start.17 = (bf16[1,4,64,8,512]{4,3,2,1,0:T(8,128)(2,1)S(1)}, bf16[1,4,64,8,512]{4,3,2,1,0:T(8,128)(2,1)}, u32[]{:S(2)}) copy-start(bf16[1,4,64,8,512]{4,3,2,1,0:T(8,128)(2,1)} %copy-done.16) | copy-start | bytes 6291460
  198.5 7.9 copy-start.54
  200.5 33.9 %all-to-all-start.3 = ((bf16[1,2,512,512]{3,1,0,2:T(2,128)(2,1)}), bf16[1,2,512,512]{3,1,0,2:T(2,128)(2,1)}, u32[]{:S(2)}, u32[]{:S(2)}) async-start(bf16[1,2,512,512]{3,1,0,2:T(2,128)(2,1)} %copy.64), calls=%async_computation.3 | async-start | bytes 2097152 | tf_op jit(solution)/shard_map/all_to_all | solution.py:235
  209.8 6.6 copy-start.18
  209.8 6.6 copy-start.23
  234.4 277.6 %all-to-all-start.4 = ((bf16[1,2,512,512]{3,1,0,2:T(2,128)(2,1)}), bf16[1,2,512,512]{3,1,0,2:T(2,128)(2,1)}, u32[]{:S(2)}, u32[]{:S(2)}) async-start(bf16[1,2,512,512]{3,1,0,2:T(2,128)(2,1)} %copy.67), calls=%async_computation.4 | async-start | bytes 2097152 | tf_op jit(solution)/shard_map/all_to_all | solution.py:235
  239.9 262.3 %all-reduce.8.cloned.1.call-start = ((), (), s32[]{:S(2)}) async-start(), calls=%async_computation.5 | async-start | bytes 1048576 | tf_op jit(solution)/shard_map/psum | solution.py:23
  241.8 5.1 copy-start.25
  241.8 5.1 copy-start.30
  241.8 5.1 copy-start.44
  241.8 5.1 copy-start.49
  241.8 940.5 %all-reduce.10.cloned.1.call-start = ((), (), s32[]{:S(2)}) async-start(), calls=%async_computation.6 | async-start | bytes 786432 | tf_op jit(solution)/shard_map/psum | solution.py:10
  527.5 3.7 copy-start.26
  527.5 3.7 copy-start.28
  527.5 3.7 copy-start.31
  527.5 3.7 copy-start.37
  527.5 3.7 copy-start.39
  531.1 745.2 %all-reduce.12.cloned.1.call-start = ((), (), s32[]{:S(2)}) async-start(), calls=%async_computation.7 | async-start | bytes 786432 | tf_op jit(solution)/shard_map/psum | solution.py:11
  531.2 748.3 %copy-start.1 = (bf16[128,512]{1,0:T(8,128)(2,1)S(1)}, bf16[128,512]{1,0:T(8,128)(2,1)}, u32[]{:S(2)}) copy-start(bf16[128,512]{1,0:T(8,128)(2,1)} %param.14) | copy-start | bytes 393220
  (35 other events, 76.5 us)
Sparse Core Ops, SparseCore 0:
  246.2 255.9 all-reduce.7
Sparse Core Ops, SparseCore 1:
  531.2 651.1 all-reduce.9
  1184.9 91.3 all-reduce.11
